TPU v7x, 128 devices: a whole 4x4x4 slice. The times are simulated.
128 devices in a mesh: expert: 16 (over z, x), tensor: 8 (over y, core).
Axes of the slice: x: 4, y: 4, z: 4, core: 2. Of those that a mesh axis runs over, the one named last changes fastest.
Arguments:
- tokens: bfloat16 [2048, 4096], P('expert'), may hold values from -6 to 6
- scores: float32 [2048, 8], P('expert'), may hold values from -6 to 6
- expert_ids: int32 [2048, 8], P('expert'), may hold values from 0 to 63, all different within a row; in each aligned block of 128 rows (0 to 127, 128 to 255, ...) at most 32 rows name the same one
- gate_weight: bfloat16 [64, 1536, 4096], P('expert', 'tensor'), may hold values from -0.09375 to 0.09375
- up_weight: bfloat16 [64, 1536, 4096], P('expert', 'tensor'), may hold values from -0.09375 to 0.09375
- down_weight: bfloat16 [64, 1536, 4096], P('expert', 'tensor'), may hold values from -0.15625 to 0.15625
Outputs:
- mixed: bfloat16 [2048, 4096], P('expert', 'tensor')
Inputs may be any that keep to these rules, and one draw needn't show every extreme that they name: `expert_ids`: each row names 8 different experts. Among the 128 rows of one owner (rows o * 128 to (o + 1) * 128 - 1) no expert is named more than 32 times.
All inputs are finite; a program needn't handle non-finite values.
Results may differ from a plain program's by a relative error of at most 0.018.
Values may be sent and summed in bfloat16 or wider, within the bound.
A program may use at most 128 MiB of HBM per device.

v0:
```python
import jax
import jax.numpy as jnp
from jax import lax
from jax.sharding import PartitionSpec as P

TOP = 8


def copy_for_each(x, axis):
    copies = jnp.broadcast_to(x, (lax.axis_size(axis), *x.shape))
    return lax.all_to_all(copies, axis, split_axis=0, concat_axis=0, tiled=True)


def in_order(parts, dim):
    dims = list(parts.shape[1:])
    dims[dim] *= parts.shape[0]
    return jnp.moveaxis(parts, 0, dim).reshape(dims)


def gathered_copies(x, axis, dim):
    parts = copy_for_each(x, axis)
    return in_order(parts, dim)


def gate_of(scores):
    lifted = jnp.exp(scores)
    return (lifted / jnp.sum(lifted, axis=-1, keepdims=True)).astype(jnp.bfloat16)


def slot_tables(expert_ids, gate_values, experts, blocks, capacity):
    rows_all = expert_ids.shape[0]
    block_rows = rows_all // blocks
    expert_count = experts.shape[0]
    matches = expert_ids[:, :, None] == experts[None, None, :]
    routed = jnp.any(matches, axis=1).astype(jnp.int32)
    chosen_gate = jnp.sum(
        jnp.where(matches, gate_values.astype(jnp.float32)[:, :, None], jnp.float32(0.0)), axis=1
    )
    folded = routed.reshape(blocks, block_rows, expert_count)
    rank_in_block = jnp.cumsum(folded, axis=1) - folded
    block_start = (jnp.arange(blocks, dtype=jnp.int32) * capacity)[:, None, None]
    slot_index = (block_start + rank_in_block).reshape(rows_all, expert_count)
    slot_index = jnp.where(routed == 1, slot_index, blocks * capacity)
    columns = jnp.broadcast_to(jnp.arange(expert_count, dtype=jnp.int32)[None, :], slot_index.shape)
    position = jnp.broadcast_to(jnp.arange(rows_all, dtype=jnp.int32)[:, None], slot_index.shape)
    slot_token = (
        jnp.full((expert_count, blocks * capacity), rows_all, jnp.int32)
        .at[columns, slot_index]
        .set(position, mode="drop")
    )
    slot_gate = (
        jnp.zeros((expert_count, blocks * capacity), jnp.float32)
        .at[columns, slot_index]
        .set(chosen_gate, mode="drop")
    )
    return (slot_token, slot_gate)


def local(tokens, scores, expert_ids, gate_weight, up_weight, down_weight):
    groups = lax.axis_size("expert")
    ranks = lax.axis_size("tensor")
    local_experts = gate_weight.shape[0]
    owner_rows = tokens.shape[0]
    width = tokens.shape[1]
    share = width // ranks
    capacity = 2 * owner_rows * TOP // (local_experts * groups)
    gate_values = gate_of(scores)
    all_ids = gathered_copies(expert_ids, "expert", 0)
    all_gates = gathered_copies(gate_values, "expert", 0)
    first_expert = lax.axis_index("expert") * local_experts
    held_experts = first_expert + jnp.arange(local_experts, dtype=jnp.int32)
    slot_token, slot_gate = slot_tables(all_ids, all_gates, held_experts, groups, capacity)
    send_order = (
        jnp.arange(local_experts, dtype=jnp.int32)[:, None]
        + local_experts * jnp.arange(groups, dtype=jnp.int32)[None, :]
    ).reshape(-1)
    send_token = slot_tables(expert_ids, gate_values, send_order, 1, capacity)[0]
    send_index = send_token.reshape(-1)
    column_start = lax.axis_index("tensor") * share
    narrow = lax.dynamic_slice_in_dim(tokens, column_start, share, 1)
    outgoing = jnp.take(narrow, send_index, axis=0, mode="fill", fill_value=0).reshape(
        local_experts, groups * capacity, share
    )
    arrived = lax.all_to_all(outgoing, "expert", split_axis=1, concat_axis=1, tiled=True)
    piece = lax.all_gather(arrived, "tensor", axis=2, tiled=True)
    gate_next = jnp.einsum("jcd,jfd->jcf", piece, gate_weight, preferred_element_type=jnp.float32)
    up_next = jnp.einsum("jcd,jfd->jcf", piece, up_weight, preferred_element_type=jnp.float32)
    hidden = (jax.nn.silu(gate_next) * up_next).astype(jnp.bfloat16)
    partial_value = jnp.einsum(
        "jcf,jfd->jcd", hidden, down_weight, preferred_element_type=jnp.float32
    ).astype(jnp.bfloat16)
    summed = lax.psum_scatter(partial_value, "tensor", scatter_dimension=2, tiled=True).astype(
        jnp.float32
    )
    gated = summed * slot_gate[:, :, None]
    returned = lax.all_to_all(
        gated.astype(jnp.bfloat16), "expert", split_axis=1, concat_axis=1, tiled=True
    ).astype(gated.dtype)
    mixed = (
        jnp.zeros((owner_rows, share), jnp.float32)
        .at[send_index]
        .add(returned.reshape(-1, share), mode="drop")
    )
    return mixed.astype(jnp.bfloat16)


def solution(mesh):
    in_specs = (
        P("expert", None),
        P("expert", None),
        P("expert", None),
        P("expert", "tensor", None),
        P("expert", "tensor", None),
        P("expert", "tensor", None),
    )
    out_specs = P("expert", "tensor")
    return jax.shard_map(local, mesh=mesh, in_specs=in_specs, out_specs=out_specs, check_vma=False)
```

profile of v0, /device:TPU:9, one launch (start us, length us, event | category | flops | bytes accessed | tf_op | source)
XLA Modules:
  0.0 370.6 jit_solution(3893563274801632213)
XLA Ops:
  6.6 0.1 add.116
  6.6 0.9 compare_reduce_fusion.1
  7.5 4.4 %copy.97 = s32[128,64,1]{2,1,0:T(8,128)} copy(s32[128,64,1]{0,1,2:T(8,128)S(1)} %convert_bitcast_fusion.2) | data formatting | bytes 65536 | tf_op jit(solution)/shard_map/convert_element_type | solution.py:35
  12.0 4.5 %fusion.14 = s32[128,64,1]{2,1,0:T(8,128)} fusion(s32[128,64,1]{2,1,0:T(8,128)} %copy.97), kind=kOutput, calls=%fused_computation.52 | output fusion | flops 1040384 | bytes 65536 | tf_op jit(solution)/shard_map/jit(cumsum)/reduce_window_sum | solution.py:40
  16.5 3.8 %copy.98 = s32[128,64,1]{0,1,2:T(8,128)S(1)} copy(s32[128,64,1]{2,1,0:T(8,128)} %fusion.14) | data formatting | bytes 65536 | tf_op jit(solution)/shard_map/jit(cumsum)/reduce_window_sum | solution.py:40
  20.3 0.1 multiply_reduce_fusion.1
  20.3 0.1 and_reduce_fusion.1
  20.4 0.1 copy.99
  20.5 0.1 reshape.257
  20.6 0.1 reshape.259
  20.7 30.4 %scatter_custom_fusion.1 = s32[2048]{0:T(1024)S(1)} fusion(s32[8192]{0:T(1024)S(1)} %reshape.257, s32[8192]{0:T(1024)S(1)} %reshape.259, s32[]{:T(128)} %constant.17.clone.1), kind=kCustom, calls=%fused_computation.41 | custom fusion | bytes 8196
  51.2 0.1 copy.100
  51.3 0.1 reshape.223
  51.4 0.1 reshape.224
  51.5 0.2 copy.102
  51.8 7.5 %gather_fusion = bf16[2048,512]{1,0:T(8,128)(2,1)S(1)} fusion(bf16[128,512]{1,0:T(8,128)(2,1)S(1)} %constant_dynamic-slice_fusion, s32[2048]{0:T(1024)S(1)} %broadcast_clamp_fusion), kind=kCustom, calls=%fused_computation | custom fusion | bytes 4202496 | tf_op jit(solution)/shard_map/jit(_take)/gather | solution.py:81
  59.3 5.2 %copy_select_fusion = bf16[4,512,512]{2,0,1:T(4,128)(2,1)S(1)} fusion(bf16[4,512,512]{2,1,0:T(8,128)(2,1)S(1)} %bitcast.45, pred[4,512]{0,1:T(8,128)(4,1)S(1)} %copy.102), kind=kLoop, calls=%fused_computation.8 | loop fusion | flops 1048576 | bytes 4196352 | tf_op jit(solution)/shard_map/jit(_take)/select_n | solution.py:81
  64.5 34.7 %all_to_all.20 = bf16[4,512,512]{2,0,1:T(4,128)(2,1)S(1)} all-to-all(bf16[4,512,512]{2,0,1:T(4,128)(2,1)S(1)} %copy_select_fusion), channel_id=1, replica_groups=mesh['expert'=16,'tensor'=8] {'expert'}, dimensions={1} | all-to-all | bytes 4194304 | tf_op jit(solution)/shard_map/all_to_all | solution.py:84
  99.2 1.8 copy.104
  101.0 84.0 %all-gather.2.cloned.1.call-done = bf16[4,512,4096]{2,1,0:T(8,128)(2,1)} async-done(((bf16[4,512,512]{2,1,0:T(8,128)(2,1)}), bf16[4,512,4096]{2,1,0:T(8,128)(2,1)}) %all-gather.2.cloned.1.call-update) | async-done | bytes 16777232 | tf_op jit(solution)/shard_map/all_gather | solution.py:85
  185.0 11.0 %fusion.16 = f32[4,512,192]{1,2,0:T(8,128)S(1)} fusion(bf16[4,512,4096]{2,1,0:T(8,128)(2,1)} %all-gather.2.cloned.1.call-done, bf16[4,192,4096]{2,1,0:T(8,128)(2,1)} %param.9), kind=kOutput, calls=%fused_computation.54 | convolution fusion | flops 3221225472 | bytes 24641536 | tf_op jit(solution)/shard_map/jcd,jfd->jcf/dot_general | solution.py:86
  196.0 21.6 %convolution_convert_fusion = bf16[4,512,4096]{2,1,0:T(8,128)(2,1)} fusion(bf16[4,192,4096]{2,1,0:T(8,128)(2,1)} %param.11, f32[4,512,192]{1,2,0:T(8,128)S(1)} %fusion.16, bf16[4,512,4096]{2,1,0:T(8,128)(2,1)} %all-gather.2.cloned.1.call-done, bf16[4,192,4096]{2,1,0:T(8,128)(2,1)} %param.10), kind=kOutput, calls=%fused_computation.4 | convolution fusion | flops 6453198848 | bytes 47710208 | tf_op jit(solution)/shard_map/jcf,jfd->jcd/dot_general | solution.py:89
  217.7 0.7 copy-done.3
  218.4 0.6 broadcast_in_dim.87
  219.0 6.7 %all-to-all-start.2 = ((bf16[16,128,8]{1,2,0:T(8,128)(2,1)}), bf16[16,128,8]{1,2,0:T(8,128)(2,1)S(1)}, u32[]{:S(2)}, u32[]{:S(2)}) async-start(bf16[16,128,8]{1,2,0:T(8,128)(2,1)} %broadcast_in_dim.87), calls=%async_computation.3 | async-start | bytes 65536 | tf_op jit(solution)/shard_map/all_to_all | solution.py:11
  225.8 6.4 %all-to-all-done.2 = bf16[16,128,8]{1,2,0:T(8,128)(2,1)S(1)} async-done(((bf16[16,128,8]{1,2,0:T(8,128)(2,1)}), bf16[16,128,8]{1,2,0:T(8,128)(2,1)S(1)}, u32[]{:S(2)}, u32[]{:S(2)}) %all-to-all-start.2) | async-done | bytes 32800 | tf_op jit(solution)/shard_map/all_to_all | solution.py:11
  232.1 0.6 broadcast_in_dim.85
  232.8 3.5 all-to-all-start.1
  236.3 6.4 %all-to-all-done.1 = s32[16,128,8]{1,2,0:T(8,128)S(1)} async-done(((s32[16,128,8]{1,2,0:T(8,128)}), s32[16,128,8]{1,2,0:T(8,128)S(1)}, u32[]{:S(2)}, u32[]{:S(2)}) %all-to-all-start.1) | async-done | bytes 65568 | tf_op jit(solution)/shard_map/all_to_all | solution.py:11
  242.7 0.2 compare_reduce_fusion
  242.9 0.5 copy.105
  243.5 23.3 %fusion.15 = s32[16,128,4]{2,0,1:T(8,128)S(1)} fusion(s32[16,128,4]{2,0,1:T(8,128)S(1)} %copy.105), kind=kOutput, calls=%fused_computation.53 | output fusion | flops 1040384 | bytes 65536 | tf_op jit(solution)/shard_map/jit(cumsum)/reduce_window_sum | solution.py:40
  266.8 0.4 copy.106
  267.3 0.1 multiply_reduce_fusion
  267.4 0.1 and_reduce_fusion
  267.5 0.4 copy.107
  267.9 0.6 reshape.263
  268.5 0.2 fusion.3
  268.7 0.4 copy.108
  269.1 0.6 reshape.265
  269.7 30.4 %scatter_custom_fusion.2 = f32[2048]{0:T(1024)S(1)} fusion(s32[8192]{0:T(1024)S(1)} %reshape.263, f32[8192]{0:T(1024)S(1)} %reshape.265, f32[]{:T(128)} %constant.16.clone.1), kind=kCustom, calls=%fused_computation.39 | custom fusion | bytes 8196
  300.2 9.2 %reduce-scatter.2.cloned.1.call-done = bf16[4,512,512]{2,1,0:T(8,128)(2,1)} async-done(((bf16[4,512,4096]{2,1,0:T(8,128)(2,1)}), bf16[4,512,512]{2,1,0:T(8,128)(2,1)}) %reduce-scatter.2.cloned.1.call-update) | async-done | bytes 2097168 | tf_op jit(solution)/shard_map/reduce_scatter | solution.py:92
  309.3 2.1 multiply_convert_fusion
  311.4 1.6 copy.109
  313.1 36.7 %all_to_all.21 = bf16[4,512,512]{2,0,1:T(4,128)(2,1)S(1)} all-to-all(bf16[4,512,512]{2,0,1:T(4,128)(2,1)S(1)} %copy.109), channel_id=1, replica_groups=mesh['expert'=16,'tensor'=8] {'expert'}, dimensions={1} | all-to-all | bytes 4194304 | tf_op jit(solution)/shard_map/all_to_all | solution.py:96
  349.8 0.4 copy.110
  350.2 12.9 %scatter_custom_fusion = f32[128,512]{1,0:T(8,128)S(1)} fusion(s32[2048]{0:T(1024)S(1)} %bitcast.52, bf16[2048,512]{1,0:T(8,128)(2,1)S(1)} %bitcast.46, f32[]{:T(128)} %constant.16.clone.1), kind=kCustom, calls=%fused_computation.5 | custom fusion | flops 2097152 | bytes 2359300 | tf_op jit(solution)/shard_map/scatter-add | solution.py:102
  363.1 0.7 convert_element_type.85
  (44 shorter events, 0.5 us)
Async XLA Ops:
  6.5 45.2 %copy-start = (bf16[128,4096]{1,0:T(8,128)(2,1)S(1)}, bf16[128,4096]{1,0:T(8,128)(2,1)}, u32[]{:S(2)}) copy-start(bf16[128,4096]{1,0:T(8,128)(2,1)} %param.6) | copy-start | bytes 3145732
  6.5 178.5 %all-gather.2.cloned.1.call-start = ((), (), s32[]{:S(2)}) async-start(), calls=%async_computation.5 | async-start | bytes 18874368 | tf_op jit(solution)/shard_map/all_gather | solution.py:85
  16.5 3.8 %copy-start.6 = (s32[2]{0:T(128)S(1)}, s32[2]{0:T(128)}, u32[]{:S(2)}) copy-start(s32[2]{0:T(128)} %constant.68) | copy-start | bytes 28
  16.5 3.9 %copy-start.7 = (s32[2]{0:T(128)S(1)}, s32[2]{0:T(128)}, u32[]{:S(2)}) copy-start(s32[2]{0:T(128)} %constant.71) | copy-start | bytes 28
  101.0 208.4 %reduce-scatter.2.cloned.1.call-start = ((), (), s32[]{:S(2)}) async-start(), calls=%async_computation.6 | async-start | bytes 18874368 | tf_op jit(solution)/shard_map/reduce_scatter | solution.py:92
  217.7 0.7 copy-start.3
  217.7 14.5 %copy-start.2 = (s32[128,8]{0,1:T(8,128)S(1)}, s32[128,8]{0,1:T(8,128)}, u32[]{:S(2)}) copy-start(s32[128,8]{0,1:T(8,128)} %param.8) | copy-start | bytes 12292
  218.3 48.9 %copy-start.5 = (s32[2]{0:T(128)S(1)}, s32[2]{0:T(128)}, u32[]{:S(2)}) copy-start(s32[2]{0:T(128)} %constant.74) | copy-start | bytes 28
  218.3 49.0 %copy-start.4 = (s32[2]{0:T(128)S(1)}, s32[2]{0:T(128)}, u32[]{:S(2)}) copy-start(s32[2]{0:T(128)} %constant.77) | copy-start | bytes 28
  219.0 13.1 %all-to-all-start.2 = ((bf16[16,128,8]{1,2,0:T(8,128)(2,1)}), bf16[16,128,8]{1,2,0:T(8,128)(2,1)S(1)}, u32[]{:S(2)}, u32[]{:S(2)}) async-start(bf16[16,128,8]{1,2,0:T(8,128)(2,1)} %broadcast_in_dim.87), calls=%async_computation.3 | async-start | bytes 65536 | tf_op jit(solution)/shard_map/all_to_all | solution.py:11
  232.8 10.0 %all-to-all-start.1 = ((s32[16,128,8]{1,2,0:T(8,128)}), s32[16,128,8]{1,2,0:T(8,128)S(1)}, u32[]{:S(2)}, u32[]{:S(2)}) async-start(s32[16,128,8]{1,2,0:T(8,128)} %broadcast_in_dim.85), calls=%async_computation.2 | async-start | bytes 131072 | tf_op jit(solution)/shard_map/all_to_all | solution.py:11
  313.0 50.7 %copy-start.1 = (bf16[128,4096]{1,0:T(8,128)(2,1)S(1)}, bf16[128,4096]{1,0:T(8,128)(2,1)}, u32[]{:S(2)}) copy-start(bf16[128,4096]{1,0:T(8,128)(2,1)} %param.6) | copy-start | bytes 3145732
Sparse Core Ops, SparseCore 0:
  101.1 83.8 all-gather.1
  217.8 91.4 reduce-scatter.1
where the time goes:
time: 371 us
  waiting for transfers between devices  106 us (29%)
  local copies, waits for them, and re-layouts  86.3 us (23%)
  blocking collectives  71.4 us (19%)
  other arithmetic  50.3 us (14%)
  matrix products  32.6 us (9%)
  between operations  13.7 us (4%)
  starting transfers between devices  10.2 us (3%)
    all_gather x1, waiting for transfers between devices, local(): piece = lax.all_gather(arrived, 'tensor', axis=2, tiled=True)  84 us
    unnamed x24, local copies, waits for them, and re-layouts  62.8 us
    all_to_all x1, blocking collectives, local(): lax.all_to_all(gated.astype(jnp.bfloat16), 'expert', split_axis=1, concat...  36.7 us
    all_to_all x1, blocking collectives, local(): lax.all_to_all(outgoing, 'expert', split_axis=1, concat_axis=1, tiled=True)  34.7 us
    another operation x2, other arithmetic, slot_tables(): rank_in_block = jnp.cumsum(folded, axis=1) - folded  27.8 us
    dot_general x1, matrix products, local(): jnp.einsum('jcf,jfd->jcd', hidden, down_weight, preferred_element_type=jn...  21.6 us
    scatter-add x1, other arithmetic, local(): mixed = jnp.zeros((owner_rows, share), jnp.float32).at[send_index].add(re...  12.9 us
    all_to_all x2, waiting for transfers between devices, copy_for_each(): return lax.all_to_all(copies, axis, split_axis=0, concat_axis=0, tiled=True)  12.8 us
  transfers between devices with their start and end apart: 4, of which 4 were waited for; matrix products, arithmetic and copies ran while one was open for 16% of the time, Pallas kernels for 0%

commit v1 on v0

--- a/solution.py
+++ b/solution.py
@@ -82,7 +82,9 @@
         local_experts, groups * capacity, share
     )
     arrived = lax.all_to_all(outgoing, "expert", split_axis=1, concat_axis=1, tiled=True)
-    piece = lax.all_gather(arrived, "tensor", axis=2, tiled=True)
+    piece = jnp.concatenate(
+        lax.all_to_all(jnp.stack([arrived] * lax.axis_size("tensor")), "tensor", 0, 0), axis=2
+    )
     gate_next = jnp.einsum("jcd,jfd->jcf", piece, gate_weight, preferred_element_type=jnp.float32)
     up_next = jnp.einsum("jcd,jfd->jcf", piece, up_weight, preferred_element_type=jnp.float32)
     hidden = (jax.nn.silu(gate_next) * up_next).astype(jnp.bfloat16)

time: 371 us -> 480 us (1.29)
  blocking collectives: 71.4 us -> 262 us
  waiting for transfers between devices: 106 us -> 21.1 us
  local copies, waits for them, and re-layouts: 86.3 us -> 93.9 us
    all_to_all x0 -> x1, blocking collectives: none -> 191 us  [local(): lax.all_to_all(jnp.stack([arrived] * lax.axis_size('tensor')), 'tensor',...]
    all_gather x1 -> x0, waiting for transfers between devices: 84 us -> none  [local(): piece = lax.all_gather(arrived, 'tensor', axis=2, tiled=True)]
    reshape x0 -> x1, local copies, waits for them, and re-layouts: none -> 7.31 us  [local(): jnp.concatenate(lax.all_to_all(jnp.stack([arrived] * lax.axis_size('tenso...]
    unnamed x24 -> x28, local copies, waits for them, and re-layouts: 62.8 us -> 62.8 us
  transfers between devices with their start and end apart: 4 -> 3, of which waited for: 4 -> 3; matrix products, arithmetic and copies ran while one was open for 16% -> 12% of each run, Pallas kernels for 0% -> 0%
where the time goes in v1:
time: 480 us; the launch traced here: 479 us
  blocking collectives  262 us (55%)
  local copies, waits for them, and re-layouts  93.9 us (20%)
  other arithmetic  50.3 us (10%)
  matrix products  30.8 us (6%)
  waiting for transfers between devices  21.1 us (4%)
  between operations  13.8 us (3%)
  starting transfers between devices  7 us (1%)
    all_to_all x1, blocking collectives, local(): lax.all_to_all(jnp.stack([arrived] * lax.axis_size('tensor')), 'tensor',...  191 us
    unnamed x28, local copies, waits for them, and re-layouts  62.8 us
    all_to_all x1, blocking collectives, local(): lax.all_to_all(gated.astype(jnp.bfloat16), 'expert', split_axis=1, concat...  36.6 us
    all_to_all x1, blocking collectives, local(): lax.all_to_all(outgoing, 'expert', split_axis=1, concat_axis=1, tiled=True)  34.7 us
    another operation x2, other arithmetic, slot_tables(): rank_in_block = jnp.cumsum(folded, axis=1) - folded  27.8 us
    dot_general x1, matrix products, local(): jnp.einsum('jcf,jfd->jcd', hidden, down_weight, preferred_element_type=jn...  21.6 us
    scatter-add x1, other arithmetic, local(): mixed = jnp.zeros((owner_rows, share), jnp.float32).at[send_index].add(re...  12.9 us
    all_to_all x2, waiting for transfers between devices, copy_for_each(): return lax.all_to_all(copies, axis, split_axis=0, concat_axis=0, tiled=True)  12.7 us
  transfers between devices with their start and end apart: 3, of which 3 were waited for; matrix products, arithmetic and copies ran while one was open for 12% of the time, Pallas kernels for 0%

profile of v1, /device:TPU:9, one launch (start us, length us, event | category | flops | bytes accessed | tf_op | source)
XLA Modules:
  0.0 479.3 jit_solution(4882100054351565070)
XLA Ops:
  6.6 0.1 add.116
  6.6 0.9 compare_reduce_fusion.1
  7.5 4.4 copy.101
  12.0 4.5 fusion.14
  16.5 3.8 copy.102
  20.3 0.1 multiply_reduce_fusion.1
  20.3 0.1 and_reduce_fusion.1
  20.4 0.1 copy.103
  20.7 30.4 %scatter_custom_fusion.1 = s32[2048]{0:T(1024)S(1)} fusion(s32[8192]{0:T(1024)S(1)} %reshape.267, s32[8192]{0:T(1024)S(1)} %reshape.269, s32[]{:T(128)} %constant.17.clone.1), kind=kCustom, calls=%fused_computation.41 | custom fusion | bytes 8196
  51.2 0.1 copy.104
  51.3 0.1 reshape.231
  51.4 0.1 reshape.232
  51.5 0.2 copy.106
  51.8 7.5 %gather_fusion = bf16[2048,512]{1,0:T(8,128)(2,1)S(1)} fusion(bf16[128,512]{1,0:T(8,128)(2,1)S(1)} %constant_dynamic-slice_fusion, s32[2048]{0:T(1024)S(1)} %broadcast_clamp_fusion), kind=kCustom, calls=%fused_computation | custom fusion | bytes 4202496 | tf_op jit(solution)/shard_map/jit(_take)/gather | solution.py:81
  59.3 5.2 %copy_select_fusion = bf16[4,512,512]{2,0,1:T(4,128)(2,1)S(1)} fusion(bf16[4,512,512]{2,1,0:T(8,128)(2,1)S(1)} %bitcast.51, pred[4,512]{0,1:T(8,128)(4,1)S(1)} %copy.106), kind=kLoop, calls=%fused_computation.8 | loop fusion | flops 1048576 | bytes 4196352 | tf_op jit(solution)/shard_map/jit(_take)/select_n | solution.py:81
  64.5 34.7 %all_to_all.25 = bf16[4,512,512]{2,0,1:T(4,128)(2,1)S(1)} all-to-all(bf16[4,512,512]{2,0,1:T(4,128)(2,1)S(1)} %copy_select_fusion), channel_id=1, replica_groups=mesh['expert'=16,'tensor'=8] {'expert'}, dimensions={1} | all-to-all | bytes 4194304 | tf_op jit(solution)/shard_map/all_to_all | solution.py:84
  99.2 0.4 copy.108
  99.6 1.6 stack.2
  101.2 191.2 %all_to_all.26 = bf16[8,4,512,512]{3,2,1,0:T(8,128)(2,1)S(1)} all-to-all(bf16[8,4,512,512]{3,2,1,0:T(8,128)(2,1)S(1)} %stack.2), channel_id=1, replica_groups=mesh['expert'=16,'tensor'=8] {'tensor'}, dimensions={0} | all-to-all | bytes 33554432 | tf_op jit(solution)/shard_map/all_to_all | solution.py:86
  292.4 7.3 %copy.116 = bf16[8,4,64,8,512]{4,3,0,2,1:T(8,128)(2,1)} copy(bf16[8,4,64,8,512]{4,3,2,1,0:T(8,128)(2,1)S(1)} %bitcast.50) | data formatting | bytes 33554432 | tf_op jit(solution)/shard_map/reshape | solution.py:85
  299.7 9.2 %fusion.16 = f32[4,512,192]{1,2,0:T(8,128)S(1)} fusion(bf16[4,512,4096]{2,1,0:T(8,128)(2,1)} %bitcast.48, bf16[4,192,4096]{2,1,0:T(8,128)(2,1)S(1)} %bitcast.54), kind=kOutput, calls=%fused_computation.54 | convolution fusion | flops 3221225472 | bytes 24641536 | tf_op jit(solution)/shard_map/jcd,jfd->jcf/dot_general | solution.py:88
  309.0 21.6 %convolution_convert_fusion = bf16[4,512,4096]{2,1,0:T(8,128)(2,1)} fusion(bf16[4,192,4096]{2,1,0:T(8,128)(2,1)} %param.11, f32[4,512,192]{1,2,0:T(8,128)S(1)} %fusion.16, bf16[4,512,4096]{2,1,0:T(8,128)(2,1)} %bitcast.49, bf16[4,192,4096]{2,1,0:T(8,128)(2,1)} %param.10), kind=kOutput, calls=%fused_computation.4 | convolution fusion | flops 6453198848 | bytes 47710208 | tf_op jit(solution)/shard_map/jcf,jfd->jcd/dot_general | solution.py:91
  330.6 0.7 copy-done.3
  331.3 0.6 broadcast_in_dim.87
  331.9 3.5 all-to-all-start.3
  335.5 6.3 %all-to-all-done.3 = bf16[16,128,8]{1,2,0:T(8,128)(2,1)S(1)} async-done(((bf16[16,128,8]{1,2,0:T(8,128)(2,1)}), bf16[16,128,8]{1,2,0:T(8,128)(2,1)S(1)}, u32[]{:S(2)}, u32[]{:S(2)}) %all-to-all-start.3) | async-done | bytes 32800 | tf_op jit(solution)/shard_map/all_to_all | solution.py:11
  341.8 0.6 broadcast_in_dim.85
  342.5 3.5 all-to-all-start.2
  346.0 6.4 %all-to-all-done.2 = s32[16,128,8]{1,2,0:T(8,128)S(1)} async-done(((s32[16,128,8]{1,2,0:T(8,128)}), s32[16,128,8]{1,2,0:T(8,128)S(1)}, u32[]{:S(2)}, u32[]{:S(2)}) %all-to-all-start.2) | async-done | bytes 65568 | tf_op jit(solution)/shard_map/all_to_all | solution.py:11
  352.4 0.2 compare_reduce_fusion
  352.6 0.5 copy.110
  353.2 23.3 %fusion.15 = s32[16,128,4]{2,0,1:T(8,128)S(1)} fusion(s32[16,128,4]{2,0,1:T(8,128)S(1)} %copy.110), kind=kOutput, calls=%fused_computation.53 | output fusion | flops 1040384 | bytes 65536 | tf_op jit(solution)/shard_map/jit(cumsum)/reduce_window_sum | solution.py:40
  376.5 0.4 copy.111
  377.0 0.1 multiply_reduce_fusion
  377.1 0.1 and_reduce_fusion
  377.2 0.4 copy.112
  377.6 0.6 reshape.273
  378.2 0.2 fusion.3
  378.4 0.4 copy.113
  378.8 0.6 reshape.275
  379.4 30.4 %scatter_custom_fusion.2 = f32[2048]{0:T(1024)S(1)} fusion(s32[8192]{0:T(1024)S(1)} %reshape.273, f32[8192]{0:T(1024)S(1)} %reshape.275, f32[]{:T(128)} %constant.16.clone.1), kind=kCustom, calls=%fused_computation.39 | custom fusion | bytes 8196
  409.9 8.4 %reduce-scatter.2.cloned.1.call-done = bf16[4,512,512]{2,1,0:T(8,128)(2,1)} async-done(((bf16[4,512,4096]{2,1,0:T(8,128)(2,1)}), bf16[4,512,512]{2,1,0:T(8,128)(2,1)}) %reduce-scatter.2.cloned.1.call-update) | async-done | bytes 2097168 | tf_op jit(solution)/shard_map/reduce_scatter | solution.py:94
  418.2 2.1 multiply_convert_fusion
  420.3 1.6 copy.114
  421.9 36.6 %all_to_all.27 = bf16[4,512,512]{2,0,1:T(4,128)(2,1)S(1)} all-to-all(bf16[4,512,512]{2,0,1:T(4,128)(2,1)S(1)} %copy.114), channel_id=1, replica_groups=mesh['expert'=16,'tensor'=8] {'expert'}, dimensions={1} | all-to-all | bytes 4194304 | tf_op jit(solution)/shard_map/all_to_all | solution.py:98
  458.5 0.4 copy.115
  458.9 12.9 %scatter_custom_fusion = f32[128,512]{1,0:T(8,128)S(1)} fusion(s32[2048]{0:T(1024)S(1)} %bitcast.60, bf16[2048,512]{1,0:T(8,128)(2,1)S(1)} %bitcast.52, f32[]{:T(128)} %constant.16.clone.1), kind=kCustom, calls=%fused_computation.5 | custom fusion | flops 2097152 | bytes 2359300 | tf_op jit(solution)/shard_map/scatter-add | solution.py:104
  471.8 0.7 convert_element_type.85
  (49 shorter events, 0.6 us)
Async XLA Ops:
  6.5 45.2 %copy-start = (bf16[128,4096]{1,0:T(8,128)(2,1)S(1)}, bf16[128,4096]{1,0:T(8,128)(2,1)}, u32[]{:S(2)}) copy-start(bf16[128,4096]{1,0:T(8,128)(2,1)} %param.6) | copy-start | bytes 3145732
  6.5 411.7 %reduce-scatter.2.cloned.1.call-start = ((), (), s32[]{:S(2)}) async-start(), calls=%async_computation.6 | async-start | bytes 18874368 | tf_op jit(solution)/shard_map/reduce_scatter | solution.py:94
  16.5 3.8 copy-start.6
  16.5 3.9 copy-start.7
  101.2 198.6 %slice-start = ((s8[6291456]{0:T(1024)(128)(4,1)}), s8[2097152]{0:T(1024)(128)(4,1)S(1)}, s32[]{:S(2)}) async-start(s8[6291456]{0:T(1024)(128)(4,1)} %bitcast.53), calls=%async_computation.7 | async-start | bytes 4194304
  292.4 7.3 %slice-start.1 = ((s8[6291456]{0:T(1024)(128)(4,1)}), s8[4194304]{0:T(1024)(128)(4,1)S(1)}, s32[]{:S(2)}) async-start(s8[6291456]{0:T(1024)(128)(4,1)} %bitcast.53), calls=%async_computation.8 | async-start | bytes 8388608
  330.6 0.7 copy-start.3
  330.6 11.2 %copy-start.2 = (s32[128,8]{0,1:T(8,128)S(1)}, s32[128,8]{0,1:T(8,128)}, u32[]{:S(2)}) copy-start(s32[128,8]{0,1:T(8,128)} %param.8) | copy-start | bytes 12292
  331.3 45.7 %copy-start.5 = (s32[2]{0:T(128)S(1)}, s32[2]{0:T(128)}, u32[]{:S(2)}) copy-start(s32[2]{0:T(128)} %constant.74) | copy-start | bytes 28
  331.3 45.8 %copy-start.4 = (s32[2]{0:T(128)S(1)}, s32[2]{0:T(128)}, u32[]{:S(2)}) copy-start(s32[2]{0:T(128)} %constant.77) | copy-start | bytes 28
  331.9 9.9 %all-to-all-start.3 = ((bf16[16,128,8]{1,2,0:T(8,128)(2,1)}), bf16[16,128,8]{1,2,0:T(8,128)(2,1)S(1)}, u32[]{:S(2)}, u32[]{:S(2)}) async-start(bf16[16,128,8]{1,2,0:T(8,128)(2,1)} %broadcast_in_dim.87), calls=%async_computation.4 | async-start | bytes 65536 | tf_op jit(solution)/shard_map/all_to_all | solution.py:11
  342.5 10.0 %all-to-all-start.2 = ((s32[16,128,8]{1,2,0:T(8,128)}), s32[16,128,8]{1,2,0:T(8,128)S(1)}, u32[]{:S(2)}, u32[]{:S(2)}) async-start(s32[16,128,8]{1,2,0:T(8,128)} %broadcast_in_dim.85), calls=%async_computation.3 | async-start | bytes 131072 | tf_op jit(solution)/shard_map/all_to_all | solution.py:11
  421.9 50.6 %copy-start.1 = (bf16[128,4096]{1,0:T(8,128)(2,1)S(1)}, bf16[128,4096]{1,0:T(8,128)(2,1)}, u32[]{:S(2)}) copy-start(bf16[128,4096]{1,0:T(8,128)(2,1)} %param.6) | copy-start | bytes 3145732
Sparse Core Ops, SparseCore 0:
  330.7 87.4 reduce-scatter.1
